TPU v7x, 32 devices: a whole 2x2x4 slice. The times are simulated.
32 devices in a mesh: grp: 2 (over y), seq: 8 (over z, x), bat: 2 (over core).
Axes of the slice: x: 2, y: 2, z: 4, core: 2. Of those that a mesh axis runs over, the one named last changes fastest.
Arguments:
- queries: bfloat16 [16, 16, 192], P(('grp', 'bat')), parts along dimension 0, may hold values from -8 to 8
- latent_cache: bfloat16 [16, 4096, 576], P('grp', 'seq'), parts along dimension 0, may hold values from -128 to 128
- cache_lengths: int32 [16], P('grp'), parts along dimension 0, may hold values from 128 to 4096, as said below
- key_weight: bfloat16 [16, 128, 512], P('bat'), may hold values from -0.5 to 0.5
- value_weight: bfloat16 [16, 512, 128], P('bat'), may hold values from -0.25 to 0.25
Outputs:
- attended: bfloat16 [16, 16, 128], P(('grp', 'bat')), parts along dimension 0
There are 2 independent parts, one for each index of `grp`. A program takes and returns all parts, laid end to end along the dimension named above; an argument that names none is the same for every part. Nothing has to cross between parts.
Inputs may be any that keep to these rules, and one draw needn't show every extreme that they name: `cache_lengths`: each entry is a multiple of 128; at least one request has all 4096 positions valid and at least one has fewer.
All inputs are finite; a program needn't handle non-finite values.
Results may differ from a plain program's by a relative error of at most 0.0085.
Values may be sent and summed in bfloat16 or wider, within the bound.
A program may use at most 64 MiB of HBM per device.

v0:
```python
import functools

import jax
import jax.numpy as jnp
from jax import lax
from jax.experimental import pallas as pl
from jax.experimental.pallas import tpu as pltpu
from jax.sharding import PartitionSpec as P

MESH = pl.DeviceIdType.MESH
masked_score = -1e30
group = 8


def iota(shape, dim):
    return lax.broadcasted_iota(jnp.int32, shape, dim)


def kernel(
    n_seq,
    lengths_far,
    queries,
    cache,
    key_weight,
    value_weight,
    out,
    lengths,
    own_q,
    other_q,
    columns,
    keys,
    values,
    got_out,
    got_stats,
    send_out,
    send_stats,
    load_sems,
    column_sems,
    query_sems,
    send_sems,
    recv_sems,
    near_sem,
    all_sem,
):
    seq = lax.axis_index("seq")
    bat = lax.axis_index("bat")
    peer = 1 - bat
    half, _, width = queries.shape
    heads, nope, latent = key_weight.shape
    depth = value_weight.shape[2]
    shard = cache.shape[2]
    pairs = half * heads
    copies = depth // pairs
    scaling = width ** (-0.5)

    barrier = pltpu.get_barrier_semaphore()

    def greet(step, _):
        far = lax.rem(seq + step, n_seq)
        pl.semaphore_signal(
            barrier, inc=1, device_id={"seq": far, "bat": 1}, device_id_type=MESH
        )
        return 0

    @pl.when(bat == 1)
    def _():
        pl.semaphore_signal(barrier, inc=1, device_id={"bat": peer}, device_id_type=MESH)

    lax.fori_loop(1, n_seq, greet, 0)

    load_q = pltpu.make_async_copy(queries, own_q, load_sems.at[0])
    load_k = pltpu.make_async_copy(key_weight, keys, load_sems.at[1])
    load_v = pltpu.make_async_copy(value_weight, values, load_sems.at[2])
    load_columns = [
        pltpu.make_async_copy(
            cache.at[(bat if i < half else peer) * half + i % half], columns.at[i], column_sems.at[i]
        )
        for i in range(2 * half)
    ]
    load_lengths = pltpu.make_async_copy(lengths_far, lengths, load_sems.at[3])
    load_q.start()
    load_lengths.start()
    load_k.start()
    for copy in load_columns[:half]:
        copy.start()
    load_v.start()
    for copy in load_columns[half:]:
        copy.start()

    def joined_rows(q_ref):
        q = q_ref[...].astype(jnp.float32)
        mine = jnp.where(bat == 0, q[:, :heads], q[:, heads:]).reshape(pairs, width)
        plain = mine[:, :nope]
        head_of = iota((pairs, nope), 0) % heads
        spread = jnp.concatenate(
            [jnp.where(head_of == h, plain, 0.0) for h in range(heads)], axis=1
        ).astype(jnp.bfloat16)
        absorbed = jnp.dot(
            spread, keys[...].reshape(heads * nope, latent), preferred_element_type=jnp.float32
        )
        return absorbed, mine[:, nope:]

    def attend(q_ref, first, owner):
        absorbed, rotary = joined_rows(q_ref)
        for copy in load_columns[first : first + half]:
            copy.wait()
        lane = iota((heads, depth), 1)
        slot = lax.rem(lane, pairs)
        row = iota((heads, depth), 0)
        maxima = jnp.zeros((heads, depth), jnp.float32)
        totals = jnp.zeros((heads, depth), jnp.float32)
        sums = []
        for i in range(half):
            piece = slice(i * heads, (i + 1) * heads)
            joined = jnp.concatenate([absorbed[piece], rotary[piece]], axis=1).astype(jnp.bfloat16)
            scores = lax.dot_general(
                joined,
                columns[first + i],
                (((1,), (0,)), ((), ())),
                preferred_element_type=jnp.float32,
            )
            left = lengths[owner * half + i] - seq * shard
            scores = jnp.where(iota(scores.shape, 1) < left, scores * scaling, masked_score)
            highest = jnp.max(scores, axis=1, keepdims=True)
            weights = jnp.exp(scores - highest)
            total = jnp.sum(weights, axis=1, keepdims=True)
            here = slot == i * heads + row
            maxima = jnp.where(here, highest, maxima)
            totals = jnp.where(here, total, totals)
            sums.append(
                lax.dot_general(
                    weights.astype(jnp.bfloat16),
                    columns[first + i, :latent],
                    (((1,), (1,)), ((), ())),
                    preferred_element_type=jnp.float32,
                )
            )
        sums = jnp.concatenate(sums, axis=0)
        stats = (
            jnp.sum(maxima, axis=0, keepdims=True),
            jnp.sum(totals, axis=0, keepdims=True),
        )
        return sums, stats

    def project(sums):
        head_of = iota((pairs, latent), 0) % heads
        spread = jnp.concatenate(
            [jnp.where(head_of == h, sums, 0.0).astype(jnp.bfloat16) for h in range(heads)], axis=1
        )
        result = jnp.dot(
            spread, values[...].reshape(heads * latent, depth), preferred_element_type=jnp.float32
        )
        return result.astype(jnp.bfloat16)

    def send(source, target, far, side, index):
        return pltpu.make_async_remote_copy(
            src_ref=source,
            dst_ref=target,
            send_sem=send_sems.at[index],
            recv_sem=recv_sems.at[index, bat],
            device_id={"seq": far, "bat": side},
            device_id_type=MESH,
        )

    @pl.when(bat == 0)
    def _():
        pl.semaphore_wait(barrier, 1)
        pl.semaphore_signal(near_sem, inc=1, device_id={"bat": peer}, device_id_type=MESH)

    @pl.when(bat == 1)
    def _():
        pl.semaphore_wait(near_sem, 1)

    swap = pltpu.make_async_remote_copy(
        src_ref=own_q,
        dst_ref=other_q,
        send_sem=query_sems.at[0],
        recv_sem=query_sems.at[1],
        device_id={"bat": peer},
        device_id_type=MESH,
    )
    load_q.wait()
    swap.start()
    load_lengths.wait()
    load_k.wait()
    sums, stats = attend(own_q, 0, bat)
    got_stats[bat, seq, 0:1] = stats[0]
    got_stats[bat, seq, 1:2] = stats[1]
    load_v.wait()
    got_out[bat, seq] = project(sums)

    @pl.when(bat == 1)
    def _():
        pl.semaphore_wait(barrier, 2 * (n_seq - 1))
        pl.semaphore_signal(all_sem, inc=1, device_id={"bat": peer}, device_id_type=MESH)

    @pl.when(bat == 0)
    def _():
        pl.semaphore_wait(all_sem, 1)

    def send_near(step, _):
        far = jnp.where(2 * seq < n_seq, n_seq - 1 - step, step)

        @pl.when(far != seq)
        def _():
            send(got_stats.at[bat, seq], got_stats.at[bat, seq], far, bat, 1).start()
            send(got_out.at[bat, seq], got_out.at[bat, seq], far, bat, 0).start()

        return 0

    lax.fori_loop(0, n_seq, send_near, 0)

    swap.wait()
    sums, stats = attend(other_q, half, peer)
    send_stats[0:1] = stats[0]
    send_stats[1:2] = stats[1]
    send_out[...] = project(sums)

    def send_far(step, _):
        far = jnp.where(2 * seq < n_seq, n_seq - 1 - step, step)
        send(send_stats, got_stats.at[bat, seq], far, peer, 1).start()
        send(send_out, got_out.at[bat, seq], far, peer, 0).start()
        return 0

    lax.fori_loop(0, n_seq, send_far, 0)

    def settle(ref, sem):
        pltpu.make_async_copy(ref, ref, sem).wait()

    few = pl.ds(0, n_seq - 1)
    settle(got_stats.at[0, few], recv_sems.at[1, bat])
    settle(got_stats.at[0], recv_sems.at[1, peer])

    lane = iota((group, depth), 1)
    sub = iota((group, depth), 0)
    picked = iota((pairs, depth), 0) == iota((pairs, depth), 1) % pairs
    coefficients = []
    for side in range(2):
        peaks, sizes = [], []
        for start in range(0, n_seq, group):
            peak = jnp.zeros((group, depth), jnp.float32)
            size = jnp.zeros((group, depth), jnp.float32)
            for j in range(group):
                peak = jnp.where(sub == j, got_stats[side, start + j, 0:1], peak)
                size = jnp.where(sub == j, got_stats[side, start + j, 1:2], size)
            peaks.append(peak)
            sizes.append(size)
        top = functools.reduce(jnp.maximum, peaks)
        top = jnp.max(top, axis=0, keepdims=True)
        factors = [jnp.exp(peak - top) for peak in peaks]
        whole = functools.reduce(jnp.add, [f * s for f, s in zip(factors, sizes)])
        whole = jnp.sum(whole, axis=0, keepdims=True)
        spread = []
        for factor in factors:
            scaled = factor / whole
            for start in range(0, group, copies):
                line = jnp.sum(
                    jnp.where(sub == start + lane // pairs, scaled, 0.0), axis=0, keepdims=True
                )
                spread.append(jnp.where(picked, line, 0.0))
        spread = jnp.concatenate(spread, axis=1)
        high = spread.astype(jnp.bfloat16)
        low = (spread - high.astype(jnp.float32)).astype(jnp.bfloat16)
        coefficients.append(jnp.concatenate([high, low], axis=0))

    settle(got_out.at[0, few], recv_sems.at[0, bat])
    settle(got_out.at[0], recv_sems.at[0, peer])
    for side in range(2):
        merged = jnp.dot(
            coefficients[side],
            got_out[side].reshape(n_seq * pairs, depth),
            preferred_element_type=jnp.float32,
        )
        merged = (merged[:pairs] + merged[pairs:]).reshape(half, heads, depth)
        out[:, side * heads : (side + 1) * heads, :] = merged.astype(jnp.bfloat16)

    both = 2 * n_seq - 1
    settle(got_stats.at[0], send_sems.at[1])
    settle(got_stats.at[0, few], send_sems.at[1])
    settle(got_out.at[0], send_sems.at[0])
    settle(got_out.at[0, few], send_sems.at[0])


def per_device(n_seq, queries, latent_cache, cache_lengths, key_weight, value_weight):
    half, all_heads, _ = queries.shape
    heads = key_weight.shape[0]
    depth = value_weight.shape[2]
    pairs = half * heads
    columns = jnp.swapaxes(latent_cache, 1, 2)
    vmem, anywhere = pltpu.VMEM, pl.BlockSpec(memory_space=pltpu.HBM)
    dma = pltpu.SemaphoreType.DMA
    operands = (cache_lengths, queries, columns, key_weight, value_weight)
    held = [pltpu.with_memory_space_constraint(x, pltpu.HBM) for x in operands]
    return pl.pallas_call(
        functools.partial(kernel, n_seq),
        out_shape=jax.ShapeDtypeStruct((half, all_heads, depth), jnp.bfloat16),
        in_specs=[anywhere] * 5,
        out_specs=pl.BlockSpec(memory_space=pltpu.VMEM),
        scratch_shapes=[
            pltpu.SMEM(cache_lengths.shape, cache_lengths.dtype),
            vmem(queries.shape, queries.dtype),
            vmem(queries.shape, queries.dtype),
            vmem(columns.shape, columns.dtype),
            vmem(key_weight.shape, key_weight.dtype),
            vmem(value_weight.shape, value_weight.dtype),
            vmem((2, n_seq, pairs, depth), jnp.bfloat16),
            vmem((2, n_seq, 2, depth), jnp.float32),
            vmem((pairs, depth), jnp.bfloat16),
            vmem((2, depth), jnp.float32),
            dma((4,)),
            dma((2 * half,)),
            dma((2,)),
            dma((2,)),
            dma((2, 2)),
            pltpu.SemaphoreType.REGULAR,
            pltpu.SemaphoreType.REGULAR,
        ],
        compiler_params=pltpu.CompilerParams(
            collective_id=0, has_side_effects=True, vmem_limit_bytes=16 << 20
        ),
    )(*held)


def solution(mesh):
    placed = (
        P(("grp", "bat"), None, None),
        P("grp", "seq", None),
        P("grp"),
        P("bat", None, None),
        P("bat", None, None),
    )
    return jax.shard_map(
        functools.partial(per_device, mesh.shape["seq"]),
        mesh=mesh,
        in_specs=placed,
        out_specs=P(("grp", "bat"), None, None),
        check_vma=False,
    )
```

profile of v0, /device:TPU:1, one launch (start us, length us, event | category | flops | bytes accessed | tf_op | source)
XLA Modules:
  0.0 14.5 jit_solution(510360157728193271)
XLA Ops:
  0.0 13.9 %shard_map.55 = bf16[4,16,128]{2,1,0:T(8,128)(2,1)S(1)} custom-call(s32[8]{0:T(128)} %lengths_far.1, bf16[4,16,192]{2,1,0:T(8,128)(2,1)} %queries.1, bf16[8,576,512]{2,1,0:T(8,128)(2,1)} %bitcast.1, bf16[8,128,512]{2,1,0:T(8,128)(2,1)} %key_weight.1, bf16[8,512,128]{2,1,0:T(8,128)(2,1)} %value_weight.1), custom_call_target="tpu_custom_call" | custom-call | tf_op jit(solution)/shard_map/pallas_call | solution.py:294
  13.9 0.6 %copy.7 = bf16[4,16,128]{2,1,0:T(8,128)(2,1)} copy(bf16[4,16,128]{2,1,0:T(8,128)(2,1)S(1)} %shard_map.55) | data formatting | bytes 32768
where the time goes:
time: 14.7 us; the launch traced here: 14.5 us
  Pallas kernels  13.9 us (95%)
  local copies, waits for them, and re-layouts  0.61 us (4%)
    pallas_call x1, Pallas kernels, per_device(): pl.pallas_call(functools.partial(kernel, n_seq), out_shape=jax.ShapeDtype...  13.9 us
    unnamed x1, local copies, waits for them, and re-layouts  0.61 us

commit v1 on v0

v1 whole, which is shorter than its diff:
```python
import functools

import jax
import jax.numpy as jnp
from jax import lax
from jax.experimental import pallas as pl
from jax.experimental.pallas import tpu as pltpu
from jax.sharding import PartitionSpec as P

MESH = pl.DeviceIdType.MESH
masked_score = -1e30
group = 8
pieces = 3
stat_rows = 8


def iota(shape, dim):
    return lax.broadcasted_iota(jnp.int32, shape, dim)


def split3(x):
    parts = []
    for _ in range(pieces):
        part = x.astype(jnp.bfloat16).astype(jnp.float32)
        parts.append(part)
        x = x - part
    return parts


def kernel(
    n_seq,
    lengths_far,
    queries,
    cache,
    key_weight,
    value_weight,
    out,
    lengths,
    own_q,
    other_q,
    columns,
    keys,
    values,
    flipped,
    got,
    sent,
    load_sems,
    column_sems,
    query_sems,
    send_sems,
    recv_sems,
    near_sem,
    all_sem,
):
    seq = lax.axis_index("seq")
    bat = lax.axis_index("bat")
    peer = 1 - bat
    half, _, width = queries.shape
    heads, nope, latent = key_weight.shape
    depth = value_weight.shape[2]
    shard = cache.shape[2]
    pairs = half * heads
    total_pairs = 2 * pairs
    copies = depth // pairs
    scaling = width ** (-0.5)

    load_q = pltpu.make_async_copy(queries, own_q, load_sems.at[0])
    load_k = pltpu.make_async_copy(key_weight, keys, load_sems.at[1])
    load_v = pltpu.make_async_copy(value_weight, values, load_sems.at[2])
    load_lengths = pltpu.make_async_copy(lengths_far, lengths, load_sems.at[3])
    load_columns = [
        pltpu.make_async_copy(
            cache.at[(bat if i < half else peer) * half + i % half], columns.at[i], column_sems.at[i]
        )
        for i in range(2 * half)
    ]
    def start_pieces(source, target, sem, parts):
        size = heads // parts
        for j in range(parts):
            piece = pl.ds(j * size, size)
            pltpu.make_async_copy(source.at[piece], target.at[piece], sem).start()

    load_q.start()
    load_lengths.start()
    start_pieces(key_weight, keys, load_sems.at[1], 8)
    for copy in load_columns:
        copy.start()
    start_pieces(value_weight, values, load_sems.at[2], 8)

    barrier = pltpu.get_barrier_semaphore()

    def greet(step, _):
        far = lax.rem(seq + step, n_seq)
        pl.semaphore_signal(
            barrier, inc=1, device_id={"seq": far, "bat": 1}, device_id_type=MESH
        )
        return 0

    @pl.when(bat == 1)
    def _():
        pl.semaphore_signal(barrier, inc=1, device_id={"bat": peer}, device_id_type=MESH)

    lax.fori_loop(1, n_seq, greet, 0)

    def joined_rows(q_ref):
        q = q_ref[...].astype(jnp.float32)
        mine = jnp.where(bat == 0, q[:, :heads], q[:, heads:]).reshape(pairs, width)
        plain = mine[:, :nope]
        head_of = iota((pairs, nope), 0) % heads
        spread = jnp.concatenate(
            [jnp.where(head_of == h, plain, 0.0) for h in range(heads)], axis=1
        ).astype(jnp.bfloat16)
        absorbed = jnp.dot(
            spread, keys[...].reshape(heads * nope, latent), preferred_element_type=jnp.float32
        )
        return jnp.concatenate([absorbed, mine[:, nope:]], axis=1)

    def score(joined, i):
        piece = joined[(i % half) * heads : (i % half + 1) * heads].astype(jnp.bfloat16)
        scores = lax.dot_general(
            piece, columns[i], (((1,), (0,)), ((), ())), preferred_element_type=jnp.float32
        )
        owner = bat if i < half else peer
        left = lengths[owner * half + i % half] - seq * shard
        return jnp.where(iota(scores.shape, 1) < left, scores * scaling, masked_score)

    def soften(scores):
        highest = jnp.max(scores, axis=1, keepdims=True)
        weights = jnp.exp(scores - highest)
        return highest, jnp.sum(weights, axis=1, keepdims=True), weights.astype(jnp.bfloat16)

    def flip(i):
        flipped[i] = columns[i, :latent].T

    def weigh(weights, i):
        return jnp.dot(weights, flipped[i], preferred_element_type=jnp.float32)

    def send(source, far, side, index):
        return pltpu.make_async_remote_copy(
            src_ref=source,
            dst_ref=got.at[bat, seq],
            send_sem=send_sems.at[index],
            recv_sem=recv_sems.at[bat],
            device_id={"seq": far, "bat": side},
            device_id_type=MESH,
        )

    @pl.when(bat == 0)
    def _():
        pl.semaphore_wait(barrier, 1)
        pl.semaphore_signal(near_sem, inc=1, device_id={"bat": peer}, device_id_type=MESH)

    @pl.when(bat == 1)
    def _():
        pl.semaphore_wait(near_sem, 1)

    swap = pltpu.make_async_remote_copy(
        src_ref=own_q,
        dst_ref=other_q,
        send_sem=query_sems.at[0],
        recv_sem=query_sems.at[1],
        device_id={"bat": peer},
        device_id_type=MESH,
    )
    load_q.wait()
    swap.start()
    load_lengths.wait()
    load_k.wait()
    joined = joined_rows(own_q)

    lane = iota((heads, depth), 1)
    slot = lax.rem(lane, pairs)
    row = iota((heads, depth), 0)
    maxima = [jnp.zeros((heads, depth), jnp.float32)] * 2
    totals = [jnp.zeros((heads, depth), jnp.float32)] * 2
    sums = []
    scores, softened = {}, {}
    steps = [(i, i + 1) for i in range(0, 2 * half, 2)]
    lag = 1
    for t in range(len(steps) + lag):
        if t < len(steps):
            if t == 1:
                swap.wait()
            for i in steps[t]:
                load_columns[i].wait()
            for i in steps[t]:
                scores[i] = score(joined if i < half else other, i)
            if t == 1:
                other = joined_rows(other_q)
            for i in steps[t]:
                flip(i)
        def softs():
            if 1 <= t <= len(steps):
                for i in steps[t - 1]:
                    highest, total, softened[i] = soften(scores[i])
                    side = i // half
                    here = slot == (i % half) * heads + row
                    maxima[side] = jnp.where(here, highest, maxima[side])
                    totals[side] = jnp.where(here, total, totals[side])
        if lag == 1:
            softs()
        if lag <= t:
            for i in steps[t - lag]:
                sums.append(weigh(softened[i], i))
        if lag == 2:
            softs()

    load_v.wait()
    sums = jnp.concatenate(sums, axis=0)
    head_of = iota((total_pairs, latent), 0) % heads
    spread = jnp.concatenate(
        [jnp.where(head_of == h, sums, 0.0).astype(jnp.bfloat16) for h in range(heads)], axis=1
    )
    result = jnp.dot(
        spread, values[...].reshape(heads * latent, depth), preferred_element_type=jnp.float32
    ).astype(jnp.bfloat16)
    stats = []
    sub = iota((stat_rows, depth), 0)
    for side in range(2):
        rows = split3(jnp.sum(maxima[side], axis=0, keepdims=True))
        rows += split3(jnp.sum(totals[side], axis=0, keepdims=True))
        tile = jnp.zeros((stat_rows, depth), jnp.float32)
        for j, line in enumerate(rows):
            tile = jnp.where(sub == j, line, tile)
        stats.append(tile.astype(jnp.bfloat16))
    got[bat, seq, :pairs] = result[:pairs]
    got[bat, seq, pairs:] = stats[0]
    sent[:pairs] = result[pairs:]
    sent[pairs:] = stats[1]

    @pl.when(bat == 1)
    def _():
        pl.semaphore_wait(barrier, 2 * (n_seq - 1))
        pl.semaphore_signal(all_sem, inc=1, device_id={"bat": peer}, device_id_type=MESH)

    @pl.when(bat == 0)
    def _():
        pl.semaphore_wait(all_sem, 1)

    def send_all(step, _):
        far = jnp.where(2 * seq < n_seq, n_seq - 1 - step, step)
        send(sent, far, peer, 1).start()

        @pl.when(far != seq)
        def _():
            send(got.at[bat, seq], far, bat, 0).start()

        return 0

    lax.fori_loop(0, n_seq, send_all, 0)

    def settle(ref, sem):
        pltpu.make_async_copy(ref, ref, sem).wait()

    few = pl.ds(0, n_seq - 1)
    settle(got.at[0, few], recv_sems.at[bat])
    settle(got.at[0], recv_sems.at[peer])

    lane = iota((group, depth), 1)
    sub = iota((group, depth), 0)
    picked = iota((pairs, depth), 0) == iota((pairs, depth), 1) % pairs
    for side in range(2):
        peaks, sizes = [], []
        for start in range(0, n_seq, group):
            peak = jnp.zeros((group, depth), jnp.float32)
            size = jnp.zeros((group, depth), jnp.float32)
            for j in range(group):
                tile = got[side, start + j, pairs:].astype(jnp.float32)
                top = jnp.sum(jnp.where(sub < pieces, tile, 0.0), axis=0, keepdims=True)
                sum_ = jnp.sum(jnp.where(sub < pieces, 0.0, tile), axis=0, keepdims=True)
                peak = jnp.where(sub == j, top, peak)
                size = jnp.where(sub == j, sum_, size)
            peaks.append(peak)
            sizes.append(size)
        top = functools.reduce(jnp.maximum, peaks)
        top = jnp.max(top, axis=0, keepdims=True)
        factors = [jnp.exp(peak - top) for peak in peaks]
        whole = functools.reduce(jnp.add, [f * s for f, s in zip(factors, sizes)])
        whole = jnp.sum(whole, axis=0, keepdims=True)
        spread = []
        for factor in factors:
            scaled = factor / whole
            for start in range(0, group, copies):
                line = jnp.sum(
                    jnp.where(sub == start + lane // pairs, scaled, 0.0), axis=0, keepdims=True
                )
                spread.append(jnp.where(picked, line, 0.0))
        spread = jnp.concatenate(spread, axis=1)
        high = spread.astype(jnp.bfloat16)
        low = (spread - high.astype(jnp.float32)).astype(jnp.bfloat16)
        merged = jnp.dot(
            jnp.concatenate([high, low], axis=0),
            got[side, :, :pairs].reshape(n_seq * pairs, depth),
            preferred_element_type=jnp.float32,
        )
        merged = (merged[:pairs] + merged[pairs:]).reshape(half, heads, depth)
        out[:, side * heads : (side + 1) * heads, :] = merged.astype(jnp.bfloat16)

    settle(got.at[0], send_sems.at[1])
    settle(got.at[0, few], send_sems.at[0])


def per_device(n_seq, queries, latent_cache, cache_lengths, key_weight, value_weight):
    half, all_heads, _ = queries.shape
    heads = key_weight.shape[0]
    depth = value_weight.shape[2]
    pairs = half * heads
    latent = key_weight.shape[2]
    shard = latent_cache.shape[1]
    columns = jnp.swapaxes(latent_cache, 1, 2)
    vmem, anywhere = pltpu.VMEM, pl.BlockSpec(memory_space=pltpu.HBM)
    dma = pltpu.SemaphoreType.DMA
    operands = (cache_lengths, queries, columns, key_weight, value_weight)
    held = [pltpu.with_memory_space_constraint(x, pltpu.HBM) for x in operands]
    return pl.pallas_call(
        functools.partial(kernel, n_seq),
        out_shape=jax.ShapeDtypeStruct((half, all_heads, depth), jnp.bfloat16),
        in_specs=[anywhere] * 5,
        out_specs=pl.BlockSpec(memory_space=pltpu.VMEM),
        scratch_shapes=[
            pltpu.SMEM(cache_lengths.shape, cache_lengths.dtype),
            vmem(queries.shape, queries.dtype),
            vmem(queries.shape, queries.dtype),
            vmem(columns.shape, columns.dtype),
            vmem(key_weight.shape, key_weight.dtype),
            vmem(value_weight.shape, value_weight.dtype),
            vmem((8, shard, latent), jnp.bfloat16),
            vmem((2, n_seq, pairs + stat_rows, depth), jnp.bfloat16),
            vmem((pairs + stat_rows, depth), jnp.bfloat16),
            dma((4,)),
            dma((2 * half,)),
            dma((2,)),
            dma((2,)),
            dma((2,)),
            pltpu.SemaphoreType.REGULAR,
            pltpu.SemaphoreType.REGULAR,
        ],
        compiler_params=pltpu.CompilerParams(
            collective_id=0, has_side_effects=True, vmem_limit_bytes=32 << 20
        ),
    )(*held)


def solution(mesh):
    placed = (
        P(("grp", "bat"), None, None),
        P("grp", "seq", None),
        P("grp"),
        P("bat", None, None),
        P("bat", None, None),
    )
    return jax.shard_map(
        functools.partial(per_device, mesh.shape["seq"]),
        mesh=mesh,
        in_specs=placed,
        out_specs=P(("grp", "bat"), None, None),
        check_vma=False,
    )
```

time: 14.7 us -> 13.2 us (0.90)
  the two profiles are of different devices: /device:TPU:1 before, /device:TPU:0 now
where the time goes in v1:
time: 13.2 us; the launch traced here: 13 us
  Pallas kernels  12.4 us (94%)
  local copies, waits for them, and re-layouts  0.61 us (5%)
    pallas_call x1, Pallas kernels, per_device(): pl.pallas_call(functools.partial(kernel, n_seq), out_shape=jax.ShapeDtype...  12.4 us
    unnamed x1, local copies, waits for them, and re-layouts  0.61 us

profile of v1, /device:TPU:0, one launch (start us, length us, event | category | flops | bytes accessed | tf_op | source)
XLA Modules:
  0.0 13.0 jit_solution(7932209149488086070)
XLA Ops:
  0.0 12.4 %shard_map.55 = bf16[4,16,128]{2,1,0:T(8,128)(2,1)S(1)} custom-call(s32[8]{0:T(128)} %lengths_far.1, bf16[4,16,192]{2,1,0:T(8,128)(2,1)} %queries.1, bf16[8,576,512]{2,1,0:T(8,128)(2,1)} %bitcast.1, bf16[8,128,512]{2,1,0:T(8,128)(2,1)} %key_weight.1, bf16[8,512,128]{2,1,0:T(8,128)(2,1)} %value_weight.1), custom_call_target="tpu_custom_call" | custom-call | tf_op jit(solution)/shard_map/pallas_call | solution.py:315
  12.4 0.6 %copy.7 = bf16[4,16,128]{2,1,0:T(8,128)(2,1)} copy(bf16[4,16,128]{2,1,0:T(8,128)(2,1)S(1)} %shard_map.55) | data formatting | bytes 32768

commit v2 on v1

--- a/solution.py
+++ b/solution.py
@@ -60,7 +60,6 @@
     depth = value_weight.shape[2]
     shard = cache.shape[2]
     pairs = half * heads
-    total_pairs = 2 * pairs
     copies = depth // pairs
     scaling = width ** (-0.5)
 
@@ -82,10 +81,12 @@
 
     load_q.start()
     load_lengths.start()
-    start_pieces(key_weight, keys, load_sems.at[1], 8)
-    for copy in load_columns:
+    start_pieces(key_weight, keys, load_sems.at[1], heads)
+    for copy in load_columns[:half]:
         copy.start()
-    start_pieces(value_weight, values, load_sems.at[2], 8)
+    start_pieces(value_weight, values, load_sems.at[2], heads)
+    for copy in load_columns[half:]:
+        copy.start()
 
     barrier = pltpu.get_barrier_semaphore()
 
@@ -127,13 +128,19 @@
     def soften(scores):
         highest = jnp.max(scores, axis=1, keepdims=True)
         weights = jnp.exp(scores - highest)
-        return highest, jnp.sum(weights, axis=1, keepdims=True), weights.astype(jnp.bfloat16)
+        return highest, jnp.sum(weights, axis=1, keepdims=True), weights
 
     def flip(i):
         flipped[i] = columns[i, :latent].T
 
     def weigh(weights, i):
-        return jnp.dot(weights, flipped[i], preferred_element_type=jnp.float32)
+        blank = jnp.zeros((heads, shard), jnp.float32)
+        rows = [weights if k == i % half else blank for k in range(half)]
+        return jnp.dot(
+            jnp.concatenate(rows, axis=0).astype(jnp.bfloat16),
+            flipped[i],
+            preferred_element_type=jnp.float32,
+        )
 
     def send(source, far, side, index):
         return pltpu.make_async_remote_copy(
@@ -168,65 +175,93 @@
     load_k.wait()
     joined = joined_rows(own_q)
 
+    def project(side):
+        stack = sums[side]
+        head_of = iota((pairs, latent), 0) % heads
+        spread = jnp.concatenate(
+            [jnp.where(head_of == h, stack, 0.0).astype(jnp.bfloat16) for h in range(heads)], axis=1
+        )
+        result = jnp.dot(
+            spread, values[...].reshape(heads * latent, depth), preferred_element_type=jnp.float32
+        )
+        sub = iota((stat_rows, depth), 0)
+        rows = split3(jnp.sum(maxima[side], axis=0, keepdims=True))
+        rows += split3(jnp.sum(totals[side], axis=0, keepdims=True))
+        tile = jnp.zeros((stat_rows, depth), jnp.float32)
+        for j, line in enumerate(rows):
+            tile = jnp.where(sub == j, line, tile)
+        return result.astype(jnp.bfloat16), tile.astype(jnp.bfloat16)
+
+    def far_of(step):
+        return jnp.where(2 * seq < n_seq, n_seq - 1 - step, step)
+
+    def send_own(step, _):
+        far = far_of(step)
+
+        @pl.when(far != seq)
+        def _():
+            send(got.at[bat, seq], far, bat, 0).start()
+
+        return 0
+
+    def send_peer(step, _):
+        send(sent, far_of(step), peer, 1).start()
+        return 0
+
     lane = iota((heads, depth), 1)
     slot = lax.rem(lane, pairs)
     row = iota((heads, depth), 0)
     maxima = [jnp.zeros((heads, depth), jnp.float32)] * 2
     totals = [jnp.zeros((heads, depth), jnp.float32)] * 2
-    sums = []
-    scores, softened = {}, {}
-    steps = [(i, i + 1) for i in range(0, 2 * half, 2)]
-    lag = 1
-    for t in range(len(steps) + lag):
-        if t < len(steps):
-            if t == 1:
-                swap.wait()
-            for i in steps[t]:
-                load_columns[i].wait()
-            for i in steps[t]:
-                scores[i] = score(joined if i < half else other, i)
-            if t == 1:
-                other = joined_rows(other_q)
-            for i in steps[t]:
-                flip(i)
-        def softs():
-            if 1 <= t <= len(steps):
-                for i in steps[t - 1]:
-                    highest, total, softened[i] = soften(scores[i])
-                    side = i // half
-                    here = slot == (i % half) * heads + row
-                    maxima[side] = jnp.where(here, highest, maxima[side])
-                    totals[side] = jnp.where(here, total, totals[side])
-        if lag == 1:
-            softs()
-        if lag <= t:
-            for i in steps[t - lag]:
-                sums.append(weigh(softened[i], i))
-        if lag == 2:
-            softs()
+    sums, scores = [None, None], {}
+
+    def arrive(items):
+        for i in items:
+            load_columns[i].wait()
+
+    def score_all(items, joined):
+        for i in items:
+            scores[i] = score(joined, i)
+
+    def flip_all(items):
+        for i in items:
+            flip(i)
+
+    def weigh_all(items):
+        weights = {}
+        for i in items:
+            side = i // half
+            highest, total, weights[i] = soften(scores[i])
+            here = slot == (i % half) * heads + row
+            maxima[side] = jnp.where(here, highest, maxima[side])
+            totals[side] = jnp.where(here, total, totals[side])
+        for i in items:
+            side = i // half
+            part = weigh(weights[i], i)
+            sums[side] = part if sums[side] is None else sums[side] + part
+
+    first, second = range(half // 2), range(half // 2, half)
+    lead, rest = (half,), range(half + 1, 2 * half)
+
+    arrive(first)
+    score_all(first, joined)
+    flip_all(first)
+
+    swap.wait()
+    arrive(second)
+    score_all(second, joined)
+    other = joined_rows(other_q)
+    flip_all(second)
+    weigh_all(first)
 
     load_v.wait()
-    sums = jnp.concatenate(sums, axis=0)
-    head_of = iota((total_pairs, latent), 0) % heads
-    spread = jnp.concatenate(
-        [jnp.where(head_of == h, sums, 0.0).astype(jnp.bfloat16) for h in range(heads)], axis=1
-    )
-    result = jnp.dot(
-        spread, values[...].reshape(heads * latent, depth), preferred_element_type=jnp.float32
-    ).astype(jnp.bfloat16)
-    stats = []
-    sub = iota((stat_rows, depth), 0)
-    for side in range(2):
-        rows = split3(jnp.sum(maxima[side], axis=0, keepdims=True))
-        rows += split3(jnp.sum(totals[side], axis=0, keepdims=True))
-        tile = jnp.zeros((stat_rows, depth), jnp.float32)
-        for j, line in enumerate(rows):
-            tile = jnp.where(sub == j, line, tile)
-        stats.append(tile.astype(jnp.bfloat16))
-    got[bat, seq, :pairs] = result[:pairs]
-    got[bat, seq, pairs:] = stats[0]
-    sent[:pairs] = result[pairs:]
-    sent[pairs:] = stats[1]
+    arrive(lead)
+    weigh_all(second)
+    score_all(lead, other)
+    result, tile = project(0)
+    got[bat, seq, :pairs] = result
+    got[bat, seq, pairs:] = tile
+    flip_all(lead)
 
     @pl.when(bat == 1)
     def _():
@@ -237,17 +272,23 @@
     def _():
         pl.semaphore_wait(all_sem, 1)
 
-    def send_all(step, _):
-        far = jnp.where(2 * seq < n_seq, n_seq - 1 - step, step)
-        send(sent, far, peer, 1).start()
-
-        @pl.when(far != seq)
-        def _():
-            send(got.at[bat, seq], far, bat, 0).start()
-
-        return 0
-
-    lax.fori_loop(0, n_seq, send_all, 0)
+    early = n_seq // 4
+    lax.fori_loop(0, early, send_own, 0)
+
+    arrive(rest)
+    score_all(rest, other)
+    flip_all(rest)
+    weigh_all((*lead, *rest))
+    result, tile = project(1)
+    sent[:pairs] = result
+    sent[pairs:] = tile
+    lax.fori_loop(0, early, send_peer, 0)
+
+    def send_both(step, _):
+        send_peer(step, 0)
+        return send_own(step, 0)
+
+    lax.fori_loop(early, n_seq, send_both, 0)
 
     def settle(ref, sem):
         pltpu.make_async_copy(ref, ref, sem).wait()
@@ -324,7 +365,7 @@
             vmem(columns.shape, columns.dtype),
             vmem(key_weight.shape, key_weight.dtype),
             vmem(value_weight.shape, value_weight.dtype),
-            vmem((8, shard, latent), jnp.bfloat16),
+            vmem((2 * half, shard, latent), columns.dtype),
             vmem((2, n_seq, pairs + stat_rows, depth), jnp.bfloat16),
             vmem((pairs + stat_rows, depth), jnp.bfloat16),
             dma((4,)),

time: 13.2 us -> 12.7 us (0.962)
  the two profiles are of different devices: /device:TPU:0 before, /device:TPU:1 now
where the time goes in v2:
time: 12.7 us; the launch traced here: 12.5 us
  Pallas kernels  11.9 us (94%)
  local copies, waits for them, and re-layouts  0.61 us (5%)
    pallas_call x1, Pallas kernels, per_device(): pl.pallas_call(functools.partial(kernel, n_seq), out_shape=jax.ShapeDtype...  11.9 us
    unnamed x1, local copies, waits for them, and re-layouts  0.61 us

profile of v2, /device:TPU:1, one launch (start us, length us, event | category | flops | bytes accessed | tf_op | source)
XLA Modules:
  0.0 12.5 jit_solution(11354482630150120187)
XLA Ops:
  0.0 11.9 %shard_map.55 = bf16[4,16,128]{2,1,0:T(8,128)(2,1)S(1)} custom-call(s32[8]{0:T(128)} %lengths_far.1, bf16[4,16,192]{2,1,0:T(8,128)(2,1)} %queries.1, bf16[8,576,512]{2,1,0:T(8,128)(2,1)} %bitcast.1, bf16[8,128,512]{2,1,0:T(8,128)(2,1)} %key_weight.1, bf16[8,512,128]{2,1,0:T(8,128)(2,1)} %value_weight.1), custom_call_target="tpu_custom_call" | custom-call | tf_op jit(solution)/shard_map/pallas_call | solution.py:356
  11.9 0.6 %copy.7 = bf16[4,16,128]{2,1,0:T(8,128)(2,1)} copy(bf16[4,16,128]{2,1,0:T(8,128)(2,1)S(1)} %shard_map.55) | data formatting | bytes 32768

commit v3 on v2

--- a/solution.py
+++ b/solution.py
@@ -11,7 +11,7 @@
 masked_score = -1e30
 group = 8
 pieces = 3
-stat_rows = 8
+stat_rows = 2 * pieces
 
 
 def iota(shape, dim):
@@ -73,6 +73,7 @@
         )
         for i in range(2 * half)
     ]
+
     def start_pieces(source, target, sem, parts):
         size = heads // parts
         for j in range(parts):
@@ -80,13 +81,13 @@
             pltpu.make_async_copy(source.at[piece], target.at[piece], sem).start()
 
     load_q.start()
-    load_lengths.start()
     start_pieces(key_weight, keys, load_sems.at[1], heads)
     for copy in load_columns[:half]:
         copy.start()
     start_pieces(value_weight, values, load_sems.at[2], heads)
     for copy in load_columns[half:]:
         copy.start()
+    load_lengths.start()
 
     barrier = pltpu.get_barrier_semaphore()
 
@@ -307,8 +308,10 @@
             size = jnp.zeros((group, depth), jnp.float32)
             for j in range(group):
                 tile = got[side, start + j, pairs:].astype(jnp.float32)
-                top = jnp.sum(jnp.where(sub < pieces, tile, 0.0), axis=0, keepdims=True)
-                sum_ = jnp.sum(jnp.where(sub < pieces, 0.0, tile), axis=0, keepdims=True)
+                top, sum_ = [
+                    functools.reduce(jnp.add, [tile[k : k + 1] for k in range(at, at + pieces)])
+                    for at in (0, pieces)
+                ]
                 peak = jnp.where(sub == j, top, peak)
                 size = jnp.where(sub == j, sum_, size)
             peaks.append(peak)
@@ -317,10 +320,10 @@
         top = jnp.max(top, axis=0, keepdims=True)
         factors = [jnp.exp(peak - top) for peak in peaks]
         whole = functools.reduce(jnp.add, [f * s for f, s in zip(factors, sizes)])
-        whole = jnp.sum(whole, axis=0, keepdims=True)
+        inverse = 1.0 / jnp.sum(whole, axis=0, keepdims=True)
         spread = []
         for factor in factors:
-            scaled = factor / whole
+            scaled = factor * inverse
             for start in range(0, group, copies):
                 line = jnp.sum(
                     jnp.where(sub == start + lane // pairs, scaled, 0.0), axis=0, keepdims=True

time: 12.7 us -> 12.6 us (level)
    pallas_call x1, Pallas kernels: 11.9 us -> 11.8 us  [per_device(): pl.pallas_call(functools.partial(kernel, n_seq), out_shape=jax.ShapeDtype...]
where the time goes in v3:
time: 12.6 us; the launch traced here: 12.4 us
  Pallas kernels  11.8 us (94%)
  local copies, waits for them, and re-layouts  0.61 us (5%)
    pallas_call x1, Pallas kernels, per_device(): pl.pallas_call(functools.partial(kernel, n_seq), out_shape=jax.ShapeDtype...  11.8 us
    unnamed x1, local copies, waits for them, and re-layouts  0.61 us

profile of v3, /device:TPU:1, one launch (start us, length us, event | category | flops | bytes accessed | tf_op | source)
XLA Modules:
  0.0 12.4 jit_solution(3633255479902253966)
XLA Ops:
  0.0 11.8 %shard_map.55 = bf16[4,16,128]{2,1,0:T(8,128)(2,1)S(1)} custom-call(s32[8]{0:T(128)} %lengths_far.1, bf16[4,16,192]{2,1,0:T(8,128)(2,1)} %queries.1, bf16[8,576,512]{2,1,0:T(8,128)(2,1)} %bitcast.1, bf16[8,128,512]{2,1,0:T(8,128)(2,1)} %key_weight.1, bf16[8,512,128]{2,1,0:T(8,128)(2,1)} %value_weight.1), custom_call_target="tpu_custom_call" | custom-call | tf_op jit(solution)/shard_map/pallas_call | solution.py:359
  11.8 0.6 %copy.7 = bf16[4,16,128]{2,1,0:T(8,128)(2,1)} copy(bf16[4,16,128]{2,1,0:T(8,128)(2,1)S(1)} %shard_map.55) | data formatting | bytes 32768

commit v4 on v3

--- a/solution.py
+++ b/solution.py
@@ -82,10 +82,10 @@
 
     load_q.start()
     start_pieces(key_weight, keys, load_sems.at[1], heads)
-    for copy in load_columns[:half]:
+    for copy in load_columns[:half + 1]:
         copy.start()
     start_pieces(value_weight, values, load_sems.at[2], heads)
-    for copy in load_columns[half:]:
+    for copy in load_columns[half + 1:]:
         copy.start()
     load_lengths.start()
 
@@ -172,7 +172,6 @@
     )
     load_q.wait()
     swap.start()
-    load_lengths.wait()
     load_k.wait()
     joined = joined_rows(own_q)
 
@@ -245,6 +244,7 @@
     lead, rest = (half,), range(half + 1, 2 * half)
 
     arrive(first)
+    load_lengths.wait()
     score_all(first, joined)
     flip_all(first)
 
@@ -273,7 +273,7 @@
     def _():
         pl.semaphore_wait(all_sem, 1)
 
-    early = n_seq // 4
+    early = n_seq // 8
     lax.fori_loop(0, early, send_own, 0)
 
     arrive(rest)
@@ -286,8 +286,8 @@
     lax.fori_loop(0, early, send_peer, 0)
 
     def send_both(step, _):
-        send_peer(step, 0)
-        return send_own(step, 0)
+        send_own(step, 0)
+        return send_peer(step, 0)
 
     lax.fori_loop(early, n_seq, send_both, 0)
 

time: 12.6 us -> 12.5 us (level)
  no operation moved by 1% of the time
where the time goes in v4:
time: 12.5 us; the launch traced here: 12.4 us
  Pallas kernels  11.7 us (94%)
  local copies, waits for them, and re-layouts  0.61 us (5%)
    pallas_call x1, Pallas kernels, per_device(): pl.pallas_call(functools.partial(kernel, n_seq), out_shape=jax.ShapeDtype...  11.7 us
    unnamed x1, local copies, waits for them, and re-layouts  0.61 us

profile of v4, /device:TPU:1, one launch (start us, length us, event | category | flops | bytes accessed | tf_op | source)
XLA Modules:
  0.0 12.4 jit_solution(18318672801765544743)
XLA Ops:
  0.0 11.7 %shard_map.55 = bf16[4,16,128]{2,1,0:T(8,128)(2,1)S(1)} custom-call(s32[8]{0:T(128)} %lengths_far.1, bf16[4,16,192]{2,1,0:T(8,128)(2,1)} %queries.1, bf16[8,576,512]{2,1,0:T(8,128)(2,1)} %bitcast.1, bf16[8,128,512]{2,1,0:T(8,128)(2,1)} %key_weight.1, bf16[8,512,128]{2,1,0:T(8,128)(2,1)} %value_weight.1), custom_call_target="tpu_custom_call" | custom-call | tf_op jit(solution)/shard_map/pallas_call | solution.py:359
  11.8 0.6 %copy.7 = bf16[4,16,128]{2,1,0:T(8,128)(2,1)} copy(bf16[4,16,128]{2,1,0:T(8,128)(2,1)S(1)} %shard_map.55) | data formatting | bytes 32768

commit v5 on v4

--- a/solution.py
+++ b/solution.py
@@ -102,8 +102,6 @@
     def _():
         pl.semaphore_signal(barrier, inc=1, device_id={"bat": peer}, device_id_type=MESH)
 
-    lax.fori_loop(1, n_seq, greet, 0)
-
     def joined_rows(q_ref):
         q = q_ref[...].astype(jnp.float32)
         mine = jnp.where(bat == 0, q[:, :heads], q[:, heads:]).reshape(pairs, width)
@@ -170,6 +168,7 @@
         device_id={"bat": peer},
         device_id_type=MESH,
     )
+    lax.fori_loop(1, n_seq, greet, 0)
     load_q.wait()
     swap.start()
     load_k.wait()

time: 12.5 us -> 12.5 us (level)
  no operation moved by 1% of the time
where the time goes in v5:
time: 12.5 us; the launch traced here: 12.4 us
  Pallas kernels  11.7 us (94%)
  local copies, waits for them, and re-layouts  0.61 us (5%)
    pallas_call x1, Pallas kernels, per_device(): pl.pallas_call(functools.partial(kernel, n_seq), out_shape=jax.ShapeDtype...  11.7 us
    unnamed x1, local copies, waits for them, and re-layouts  0.61 us

profile of v5, /device:TPU:1, one launch (start us, length us, event | category | flops | bytes accessed | tf_op | source)
XLA Modules:
  0.0 12.4 jit_solution(1542232644923419782)
XLA Ops:
  0.0 11.7 %shard_map.55 = bf16[4,16,128]{2,1,0:T(8,128)(2,1)S(1)} custom-call(s32[8]{0:T(128)} %lengths_far.1, bf16[4,16,192]{2,1,0:T(8,128)(2,1)} %queries.1, bf16[8,576,512]{2,1,0:T(8,128)(2,1)} %bitcast.1, bf16[8,128,512]{2,1,0:T(8,128)(2,1)} %key_weight.1, bf16[8,512,128]{2,1,0:T(8,128)(2,1)} %value_weight.1), custom_call_target="tpu_custom_call" | custom-call | tf_op jit(solution)/shard_map/pallas_call | solution.py:358
  11.8 0.6 %copy.7 = bf16[4,16,128]{2,1,0:T(8,128)(2,1)} copy(bf16[4,16,128]{2,1,0:T(8,128)(2,1)S(1)} %shard_map.55) | data formatting | bytes 32768
